TPU v7x, 32 devices: a whole 2x2x4 slice. The times are simulated.
32 devices in a mesh: left: 8 (over z, x), right: 4 (over y, core).
Axes of the slice: x: 2, y: 2, z: 4, core: 2. Of those that a mesh axis runs over, the one named last changes fastest.
Arguments:
- density: float32 [128, 128, 2048], P(None, 'left', 'right'), may hold values from -6 to 6
- symbol_x: float32 [128], replicated, may hold values from 0.3 to 3
- symbol_y: float32 [128], replicated, may hold values from 0.3 to 3
- symbol_z: float32 [2048], replicated, may hold values from 0.3 to 3
Outputs:
- spectrum: float32 [128, 128, 2048], P('left', 'right')
All inputs are finite; a program needn't handle non-finite values.
Results may differ from a plain program's by a relative error of at most 0.00007.
Values sent between devices are 32-bit elements; how exact they have to be, the bound alone decides.
A program may use at most 192 MiB of HBM per device.

v0:
```python
import jax
import jax.numpy as jnp
from jax import lax
from jax.sharding import PartitionSpec as P


def mode_table(count):
    rank = jnp.arange(count)
    angle = 2.0 * jnp.pi / count * (rank[:, None] * rank[None, :] % count).astype(jnp.float32)
    return (jnp.cos(angle) + jnp.sin(angle)) * count ** (-0.5)


def transform_dim(values, dim):
    moved = jnp.tensordot(
        values, mode_table(values.shape[dim]), axes=([dim], [0]), precision=lax.Precision.HIGHEST
    )
    return jnp.moveaxis(moved, -1, dim)


def per_device(density, symbol_x, symbol_y, symbol_z):
    part_values = density
    part_values = transform_dim(part_values, 0)
    part_values = lax.all_to_all(part_values, "left", split_axis=0, concat_axis=1, tiled=True)
    part_values = transform_dim(part_values, 1)
    block_values = part_values
    block_values = lax.all_to_all(block_values, "right", split_axis=1, concat_axis=2, tiled=True)
    block_values = transform_dim(block_values, 2)
    share_x = block_values.shape[0]
    part_x = lax.dynamic_slice_in_dim(symbol_x, lax.axis_index("left") * share_x, share_x)
    share_y = block_values.shape[1]
    part_y = lax.dynamic_slice_in_dim(symbol_y, lax.axis_index("right") * share_y, share_y)
    symbol = part_x[:, None, None] + part_y[None, :, None] + symbol_z[None, None, :]
    block_values = block_values * lax.rsqrt(symbol)
    return block_values


def solution(mesh):
    return jax.shard_map(
        per_device,
        mesh=mesh,
        in_specs=(P(None, "left", "right"), P(), P(), P()),
        out_specs=P("left", "right", None),
        check_vma=False,
    )
```

profile of v0, /device:TPU:0, one launch (start us, length us, event | category | flops | bytes accessed | tf_op | source)
XLA Modules:
  0.0 245.7 jit_solution(8625823502980636644)
XLA Ops:
  0.0 9.0 %fusion.19 = f32[128,16,512]{2,0,1:T(8,128)S(1)} fusion(f32[128,16,512]{2,1,0:T(8,128)} %param.4), kind=kOutput, calls=%fused_computation.20 | convolution fusion | flops 1610874880 | bytes 8388608 | tf_op jit(solution)/shard_map/dot_general | solution.py:14
  9.0 2.4 copy.24
  11.5 100.3 %all_to_all.36 = f32[128,16,512]{2,1,0:T(8,128)S(1)} all-to-all(f32[128,16,512]{2,1,0:T(8,128)S(1)} %copy.24), channel_id=1, replica_groups=mesh['left'=8,'right'=4] {'left'}, dimensions={0} | all-to-all | bytes 8388608 | tf_op jit(solution)/shard_map/all_to_all | solution.py:23
  111.7 0.8 copy.25
  112.6 8.6 %convolution_bitcast_fusion = f32[16,128,512]{1,2,0:T(8,128)} fusion(f32[16,128,512]{2,1,0:T(8,128)S(1)} %bitcast.28), kind=kOutput, calls=%fused_computation.23 | convolution fusion | flops 1610874880 | bytes 8388608 | tf_op jit(solution)/shard_map/dot_general | solution.py:14
  121.2 5.5 %copy.27 = f32[16,128,512]{2,0,1:T(8,128)} copy(f32[16,128,512]{1,2,0:T(8,128)} %convolution_bitcast_fusion) | data formatting | bytes 8388608 | tf_op jit(solution)/shard_map/transpose | solution.py:17
  126.7 0.0 copy-start.1
  126.7 0.0 copy-start.2
  126.7 5.1 %all-to-all-start.1 = ((f32[16,128,512]{2,0,1:T(8,128)}), f32[16,128,512]{2,0,1:T(8,128)}, u32[]{:S(2)}, u32[]{:S(2)}) async-start(f32[16,128,512]{2,0,1:T(8,128)} %copy.27), calls=%async_computation.1 | async-start | bytes 8388608 | tf_op jit(solution)/shard_map/all_to_all | solution.py:26
  131.8 0.0 copy-done.1
  131.9 0.1 dynamic_slice.7
  131.9 0.0 copy-done.2
  131.9 0.1 dynamic_slice.6
  132.0 0.1 broadcast_add_fusion
  132.1 67.7 %fusion.51 = f32[2048,2048,1]{1,0,2:T(8,128)} fusion(), kind=kLoop, calls=%fused_computation.7.clone.clone.clone.1 | loop fusion | flops 67108864 | bytes 16777216 | tf_op jit(solution)/shard_map/dot_general | solution.py:14
  199.8 0.0 all-to-all-done.1
  199.8 6.9 %copy.29 = f32[16,32,4,512]{3,2,1,0:T(4,128)} copy(f32[16,32,4,512]{3,0,1,2:T(8,128)} %bitcast.8) | data formatting | bytes 8388608 | tf_op jit(solution)/shard_map/all_to_all | solution.py:26
  206.7 0.0 copy-start
  206.7 6.1 %all_to_all.33 = f32[16,32,2048]{2,1,0:T(8,128)} reshape(f32[16,32,4,512]{3,2,1,0:T(4,128)} %copy.29) | data formatting | bytes 8388608 | tf_op jit(solution)/shard_map/all_to_all | solution.py:26
  212.7 0.0 copy-done
  212.8 33.0 %rsqrt_multiply_fusion = f32[16,32,2048]{2,1,0:T(8,128)} fusion(f32[16,32,2048]{2,1,0:T(8,128)} %all_to_all.33, f32[2048]{0:T(1024)S(1)} %copy-done, f32[16,32]{1,0:T(8,128)S(1)} %broadcast_add_fusion, f32[2048,2048,1]{1,0,2:T(8,128)} %fusion.51), kind=kOutput, calls=%fused_computation.22 | convolution fusion | flops 25771900928 | bytes 25176064 | tf_op jit(solution)/shard_map/dot_general | solution.py:14
Async XLA Ops:
  126.7 5.2 %copy-start.1 = (f32[128]{0:T(128)S(1)}, f32[128]{0:T(128)}, u32[]{:S(2)}) copy-start(f32[128]{0:T(128)} %param.6) | copy-start | bytes 1540
  126.7 5.3 %copy-start.2 = (f32[128]{0:T(128)S(1)}, f32[128]{0:T(128)}, u32[]{:S(2)}) copy-start(f32[128]{0:T(128)} %param.5) | copy-start | bytes 1540
  126.7 73.1 %all-to-all-start.1 = ((f32[16,128,512]{2,0,1:T(8,128)}), f32[16,128,512]{2,0,1:T(8,128)}, u32[]{:S(2)}, u32[]{:S(2)}) async-start(f32[16,128,512]{2,0,1:T(8,128)} %copy.27), calls=%async_computation.1 | async-start | bytes 8388608 | tf_op jit(solution)/shard_map/all_to_all | solution.py:26
  206.7 6.1 %copy-start = (f32[2048]{0:T(1024)S(1)}, f32[2048]{0:T(1024)}, u32[]{:S(2)}) copy-start(f32[2048]{0:T(1024)} %param.7) | copy-start | bytes 24580
where the time goes:
time: 246 us
  blocking collectives  100 us (41%)
  other arithmetic  67.8 us (28%)
  matrix products  50.6 us (21%)
  local copies, waits for them, and re-layouts  21.9 us (9%)
  starting transfers between devices  5.15 us (2%)
    all_to_all x1, blocking collectives, per_device(): lax.all_to_all(part_values, 'left', split_axis=0, concat_axis=1, tiled=True)  100 us
    dot_general x1, other arithmetic, transform_dim(): jnp.tensordot(values, mode_table(values.shape[dim]), axes=([dim], [0]), p...  67.7 us
    dot_general x3, matrix products, transform_dim(): jnp.tensordot(values, mode_table(values.shape[dim]), axes=([dim], [0]), p...  50.6 us
    all_to_all x2, local copies, waits for them, and re-layouts, per_device(): lax.all_to_all(block_values, 'right', split_axis=1, concat_axis=2, tiled=...  13 us
    transpose x1, local copies, waits for them, and re-layouts, transform_dim(): return jnp.moveaxis(moved, -1, dim)  5.51 us
    all_to_all x1, starting transfers between devices, per_device(): lax.all_to_all(block_values, 'right', split_axis=1, concat_axis=2, tiled=...  5.15 us
  transfers between devices with their start and end apart: 1, of which 0 were waited for; matrix products, arithmetic and copies ran while one was open for 28% of the time, Pallas kernels for 0%

commit v1 on v0

--- a/solution.py
+++ b/solution.py
@@ -23,7 +23,12 @@
     part_values = lax.all_to_all(part_values, "left", split_axis=0, concat_axis=1, tiled=True)
     part_values = transform_dim(part_values, 1)
     block_values = part_values
-    block_values = lax.all_to_all(block_values, "right", split_axis=1, concat_axis=2, tiled=True)
+    block_values = jnp.concatenate(
+        lax.all_to_all(
+            jnp.stack(jnp.split(block_values, lax.axis_size("right"), axis=1)), "right", 0, 0
+        ),
+        axis=2,
+    )
     block_values = transform_dim(block_values, 2)
     share_x = block_values.shape[0]
     part_x = lax.dynamic_slice_in_dim(symbol_x, lax.axis_index("left") * share_x, share_x)

time: 246 us -> 227 us (0.923)
  local copies, waits for them, and re-layouts: 21.9 us -> 6.86 us
  matrix products: 50.6 us -> 43.9 us
  other arithmetic: 67.8 us -> 70.3 us
    all_to_all x2 -> x0, local copies, waits for them, and re-layouts: 13 us -> none  [per_device(): lax.all_to_all(block_values, 'right', split_axis=1, concat_axis=2, tiled=...]
    dot_general x3, matrix products: 50.6 us -> 43.9 us  [transform_dim(): jnp.tensordot(values, mode_table(values.shape[dim]), axes=([dim], [0]), p...]
    transpose x1 -> x0, local copies, waits for them, and re-layouts: 5.51 us -> none  [transform_dim(): return jnp.moveaxis(moved, -1, dim)]
    reshape x0 -> x1, local copies, waits for them, and re-layouts: none -> 2.64 us  [per_device(): jnp.concatenate(lax.all_to_all(jnp.stack(jnp.split(block_values, lax.axis...]
    another operation x0 -> x1, other arithmetic: none -> 2.52 us  [per_device(): jnp.stack(jnp.split(block_values, lax.axis_size('right'), axis=1))]
  transfers between devices with their start and end apart: 1 -> 1, of which waited for: 0 -> 0; matrix products, arithmetic and copies ran while one was open for 28% -> 30% of each run, Pallas kernels for 0% -> 0%
where the time goes in v1:
time: 227 us
  blocking collectives  100 us (44%)
  other arithmetic  70.3 us (31%)
  matrix products  43.9 us (19%)
  local copies, waits for them, and re-layouts  6.86 us (3%)
  starting transfers between devices  5.2 us (2%)
    all_to_all x1, blocking collectives, per_device(): lax.all_to_all(part_values, 'left', split_axis=0, concat_axis=1, tiled=True)  100 us
    dot_general x1, other arithmetic, transform_dim(): jnp.tensordot(values, mode_table(values.shape[dim]), axes=([dim], [0]), p...  67.7 us
    dot_general x3, matrix products, transform_dim(): jnp.tensordot(values, mode_table(values.shape[dim]), axes=([dim], [0]), p...  43.9 us
    all_to_all x1, starting transfers between devices, per_device(): lax.all_to_all(jnp.stack(jnp.split(block_values, lax.axis_size('right'),...  5.2 us
  transfers between devices with their start and end apart: 1, of which 0 were waited for; matrix products, arithmetic and copies ran while one was open for 30% of the time, Pallas kernels for 0%

profile of v1, /device:TPU:0, one launch (start us, length us, event | category | flops | bytes accessed | tf_op | source)
XLA Modules:
  0.0 226.6 jit_solution(9537511097673726067)
XLA Ops:
  0.0 8.4 %fusion.19 = f32[128,16,512]{2,0,1:T(8,128)S(1)} fusion(f32[128,16,512]{2,1,0:T(8,128)} %param.4), kind=kOutput, calls=%fused_computation.21 | convolution fusion | flops 1610874880 | bytes 8388608 | tf_op jit(solution)/shard_map/dot_general | solution.py:14
  8.5 2.4 %copy.11 = f32[128,16,512]{2,1,0:T(8,128)S(1)} copy(f32[128,16,512]{2,0,1:T(8,128)S(1)} %fusion.19) | data formatting | bytes 8388608 | tf_op jit(solution)/shard_map/dot_general | solution.py:14
  10.9 100.3 %all_to_all.23 = f32[128,16,512]{2,1,0:T(8,128)S(1)} all-to-all(f32[128,16,512]{2,1,0:T(8,128)S(1)} %copy.11), channel_id=1, replica_groups=mesh['left'=8,'right'=4] {'left'}, dimensions={0} | all-to-all | bytes 8388608 | tf_op jit(solution)/shard_map/all_to_all | solution.py:23
  111.2 0.8 copy.12
  112.0 4.7 %convolution_bitcast_fusion = f32[16,128,512]{2,1,0:T(8,128)S(1)} fusion(f32[16,128,512]{2,1,0:T(8,128)S(1)} %bitcast.35), kind=kOutput, calls=%fused_computation.24 | convolution fusion | flops 1610874880 | bytes 8388608 | tf_op jit(solution)/shard_map/dot_general | solution.py:14
  116.7 0.8 slice_bitcast_fusion.3
  117.5 2.5 %pad_maximum_fusion = f32[4,16,32,512]{3,2,1,0:T(8,128)} fusion(f32[1,16,32,512]{3,2,1,0:T(8,128)S(1)} %get-tuple-element.6, f32[1,16,32,512]{3,2,1,0:T(8,128)S(1)} %get-tuple-element.7, f32[1,16,32,512]{3,2,1,0:T(8,128)S(1)} %get-tuple-element.8, f32[1,16,32,512]{3,2,1,0:T(8,128)S(1)} %get-tuple-element.5), kind=kLoop, calls=%fused_computation.20 | loop fusion | flops 3145728 | bytes 8388608 | tf_op jit(solution)/shard_map/stack | solution.py:28
  120.0 0.0 copy-start.1
  120.0 0.0 copy-start.2
  120.0 5.2 %all-to-all-start.1 = ((f32[4,16,32,512]{3,2,1,0:T(8,128)}), f32[4,16,32,512]{3,2,1,0:T(8,128)}, u32[]{:S(2)}, u32[]{:S(2)}) async-start(f32[4,16,32,512]{3,2,1,0:T(8,128)} %pad_maximum_fusion), calls=%async_computation.1 | async-start | bytes 8388608 | tf_op jit(solution)/shard_map/all_to_all | solution.py:27
  125.3 0.0 copy-done.1
  125.3 0.1 dynamic_slice.7
  125.4 0.0 copy-done.2
  125.4 0.1 dynamic_slice.6
  125.4 0.1 broadcast_add_fusion
  125.5 67.7 %fusion.51 = f32[2048,2048,1]{1,0,2:T(8,128)} fusion(), kind=kLoop, calls=%fused_computation.7.clone.clone.clone.1 | loop fusion | flops 67108864 | bytes 16777216 | tf_op jit(solution)/shard_map/dot_general | solution.py:14
  193.2 0.0 all-to-all-done.1
  193.2 0.0 copy-start
  193.2 2.6 %copy.14 = f32[4,16,4,8,512]{4,3,0,2,1:T(8,128)S(1)} copy(f32[4,16,4,8,512]{4,3,2,1,0:T(8,128)} %bitcast.12) | data formatting | bytes 8388608 | tf_op jit(solution)/shard_map/reshape | solution.py:26
  195.8 0.0 copy-done
  195.8 30.7 %rsqrt_multiply_fusion = f32[16,32,2048]{2,1,0:T(8,128)} fusion(f32[16,32,2048]{2,1,0:T(8,128)S(1)} %bitcast.36, f32[2048]{0:T(1024)S(1)} %copy-done, f32[16,32]{1,0:T(8,128)S(1)} %broadcast_add_fusion, f32[2048,2048,1]{1,0,2:T(8,128)} %fusion.51), kind=kOutput, calls=%fused_computation.23 | convolution fusion | flops 25771900928 | bytes 25176064 | tf_op jit(solution)/shard_map/dot_general | solution.py:14
Async XLA Ops:
  120.0 5.2 %copy-start.1 = (f32[128]{0:T(128)S(1)}, f32[128]{0:T(128)}, u32[]{:S(2)}) copy-start(f32[128]{0:T(128)} %param.6) | copy-start | bytes 1540
  120.0 5.3 %copy-start.2 = (f32[128]{0:T(128)S(1)}, f32[128]{0:T(128)}, u32[]{:S(2)}) copy-start(f32[128]{0:T(128)} %param.5) | copy-start | bytes 1540
  120.0 73.1 %all-to-all-start.1 = ((f32[4,16,32,512]{3,2,1,0:T(8,128)}), f32[4,16,32,512]{3,2,1,0:T(8,128)}, u32[]{:S(2)}, u32[]{:S(2)}) async-start(f32[4,16,32,512]{3,2,1,0:T(8,128)} %pad_maximum_fusion), calls=%async_computation.1 | async-start | bytes 8388608 | tf_op jit(solution)/shard_map/all_to_all | solution.py:27
  193.2 2.6 %copy-start = (f32[2048]{0:T(1024)S(1)}, f32[2048]{0:T(1024)}, u32[]{:S(2)}) copy-start(f32[2048]{0:T(1024)} %param.7) | copy-start | bytes 24580
